TPU v7x, 32 devices: a whole 2x2x4 slice. The times are simulated.
32 devices in a mesh: island: 4 (over y, core), shard: 8 (over z, x).
Axes of the slice: x: 2, y: 2, z: 4, core: 2. Of those that a mesh axis runs over, the one named last changes fastest.
Arguments:
- pseudo_grad: float32 [4, 2048, 4096], P('island', 'shard'), may hold values from -6 to 6
- error_buffer: float32 [4, 2048, 4096], P('island', 'shard'), may hold values from -6 to 6
- momentum: float32 [2048, 4096], P('shard'), may hold values from -4 to 4
- weights: bfloat16 [2048, 4096], P('shard'), may hold values from -6 to 6
- warm_basis: float32 [2048, 64], P('shard'), may hold values from -6 to 6
Outputs:
- new_error: float32 [4, 2048, 4096], P('island', 'shard')
- new_momentum: float32 [2048, 4096], P('shard')
- new_weights: bfloat16 [2048, 4096], P('shard')
- new_basis: float32 [2048, 64], P('shard')
All inputs are finite; a program needn't handle non-finite values.
Results may differ from a plain program's by a relative error of at most 0.001.
Values sent between devices are 32-bit elements; how exact they have to be, the bound alone decides.
A program may use at most 128 MiB of HBM per device.

v0:
```python
import jax
import jax.numpy as jnp
from jax import lax
from jax.sharding import PartitionSpec as P

ITERS = 2


HIGH = lax.Precision.HIGHEST
outer_beta = 0.9
outer_rate = 0.7


def orthonormal(factor_rows):
    gram_matrix = jnp.dot(factor_rows, factor_rows.T, precision=HIGH)
    lower_factor = jnp.linalg.cholesky(gram_matrix)
    return lax.linalg.triangular_solve(lower_factor, factor_rows, left_side=True, lower=True)


def on_device(pseudo_grad, error_buffer, momentum, weights, warm_basis):
    merged = (pseudo_grad + error_buffer)[0]
    basis_now = warm_basis
    for iteration in range(ITERS):
        partial_value = lax.dot_general(basis_now, merged, (((0,), (0,)), ((), ())), precision=HIGH)
        factor_rows = orthonormal(lax.psum(partial_value, ("island", "shard")))
        local_proj = lax.dot_general(merged, factor_rows, (((1,), (1,)), ((), ())), precision=HIGH)
        basis_now = lax.psum(local_proj, "island")
    new_error = merged - jnp.dot(local_proj, factor_rows, precision=HIGH)
    update = jnp.dot(basis_now / lax.axis_size("island"), factor_rows, precision=HIGH)
    new_momentum = outer_beta * momentum + update
    stepped = weights.astype(jnp.float32) - outer_rate * (update + outer_beta * new_momentum)
    return (new_error[None], new_momentum, stepped.astype(jnp.bfloat16), basis_now)


def solution(mesh):
    in_specs = (
        P("island", "shard", None),
        P("island", "shard", None),
        P("shard", None),
        P("shard", None),
        P("shard", None),
    )
    out_specs = (P("island", "shard", None), P("shard", None), P("shard", None), P("shard", None))
    return jax.shard_map(
        on_device, mesh=mesh, in_specs=in_specs, out_specs=out_specs, check_vma=False
    )
```

profile of v0, /device:TPU:25, one launch (start us, length us, event | category | flops | bytes accessed | tf_op | source)
XLA Modules:
  0.0 417.2 jit_solution(8857783116008560494)
XLA Ops:
  7.2 0.0 copy-start
  7.2 0.0 all-reduce.5.cloned.1.call-start
  7.2 3.9 add.25
  11.2 0.0 copy-start.1
  11.2 2.0 copy-done.1
  13.2 0.0 copy-done
  13.2 3.8 convolution_bitcast_fusion
  17.0 0.0 all-reduce.5.cloned.1.call-update
  17.1 0.0 all-reduce.7.cloned.1.call-start
  17.1 129.1 %all-reduce.5.cloned.1.call-done = f32[64,4096]{1,0:T(8,128)} async-done(((f32[64,4096]{1,0:T(8,128)}), f32[64,4096]{1,0:T(8,128)}) %all-reduce.5.cloned.1.call-update) | async-done | bytes 1048592 | tf_op jit(solution)/shard_map/psum | solution.py:25
  146.2 2.5 fusion.22
  148.7 0.1 copy.9
  148.8 5.8 %cholesky.44 = f32[64,64]{1,0:T(8,128)S(1)} custom-call(f32[64,64]{1,0:T(8,128)S(1)} %fusion.17), custom_call_target="Cholesky" | custom-call | tf_op jit(solution)/shard_map/jit(cholesky)/cholesky | solution.py:16
  154.7 0.6 compare_reduce_fusion.1
  155.3 0.7 fusion.10
  156.0 4.9 %custom-call.6 = f32[1,64,64]{1,2,0:T(8,128)S(1)} custom-call(f32[1,64,64]{2,1,0:T(8,128)S(1)} %fusion.10), custom_call_target="InvertDiagBlocksLowerTriangular" | custom-call | tf_op jit(solution)/shard_map/triangular_solve/custom-call.0 | solution.py:17
  160.9 2.3 fusion.15
  163.1 5.8 %fusion.5 = f32[256,64]{1,0:T(8,128)} fusion(f32[64,4096]{1,0:T(8,128)S(1)} %fusion.15, f32[1,256,4096]{2,1,0:T(8,128)} %copy-done.1), kind=kOutput, calls=%fused_computation.7 | convolution fusion | flops 805306368 | bytes 5308416 | tf_op jit(solution)/shard_map/dot_general | solution.py:26
  169.0 0.0 all-reduce.7.cloned.1.call-update
  169.0 0.2 all-reduce.9.cloned.1.call-start
  169.2 32.4 %all-reduce.7.cloned.1.call-done = f32[256,64]{1,0:T(8,128)} async-done(((f32[256,64]{1,0:T(8,128)}), f32[256,64]{1,0:T(8,128)}) %all-reduce.7.cloned.1.call-update) | async-done | bytes 65552 | tf_op jit(solution)/shard_map/psum | solution.py:27
  201.6 5.9 %fusion.3 = f32[64,4096]{1,0:T(8,128)} fusion(f32[256,64]{1,0:T(8,128)} %all-reduce.7.cloned.1.call-done, f32[1,256,4096]{2,1,0:T(8,128)} %copy-done.1), kind=kOutput, calls=%fused_computation.5 | convolution fusion | flops 805306368 | bytes 5308416 | tf_op jit(solution)/shard_map/dot_general | solution.py:24
  207.5 0.0 all-reduce.9.cloned.1.call-update
  207.5 129.2 %all-reduce.9.cloned.1.call-done = f32[64,4096]{1,0:T(8,128)} async-done(((f32[64,4096]{1,0:T(8,128)}), f32[64,4096]{1,0:T(8,128)}) %all-reduce.9.cloned.1.call-update) | async-done | bytes 1048592 | tf_op jit(solution)/shard_map/psum | solution.py:25
  336.7 2.5 fusion.23
  339.2 0.1 copy.10
  339.3 5.8 %cholesky.55 = f32[64,64]{1,0:T(8,128)S(1)} custom-call(f32[64,64]{1,0:T(8,128)S(1)} %fusion.14), custom_call_target="Cholesky" | custom-call | tf_op jit(solution)/shard_map/jit(cholesky)/cholesky | solution.py:16
  345.2 0.6 compare_reduce_fusion
  345.8 0.7 fusion.11
  346.5 4.9 %custom-call.7 = f32[1,64,64]{1,2,0:T(8,128)S(1)} custom-call(f32[1,64,64]{2,1,0:T(8,128)S(1)} %fusion.11), custom_call_target="InvertDiagBlocksLowerTriangular" | custom-call | tf_op jit(solution)/shard_map/triangular_solve/custom-call.0 | solution.py:17
  351.4 2.3 fusion.12
  353.7 6.1 %fusion.1 = f32[256,64]{0,1:T(8,128)S(1)} fusion(f32[64,4096]{1,0:T(8,128)S(1)} %fusion.12, f32[1,256,4096]{2,1,0:T(8,128)} %copy-done.1), kind=kOutput, calls=%fused_computation.3 | convolution fusion | flops 805306368 | bytes 5308416 | tf_op jit(solution)/shard_map/dot_general | solution.py:26
  359.8 0.0 copy-start.3
  359.8 0.0 copy-start.2
  359.8 6.8 %fusion = f32[1,256,4096]{2,1,0:T(8,128)} fusion(f32[256,64]{0,1:T(8,128)S(1)} %fusion.1, f32[64,4096]{1,0:T(8,128)S(1)} %fusion.12, f32[1,256,4096]{2,1,0:T(8,128)} %copy-done.1), kind=kOutput, calls=%fused_computation.1 | convolution fusion | flops 806354944 | bytes 9502720 | tf_op jit(solution)/shard_map/dot_general | solution.py:28
  366.6 0.0 copy-done.3
  366.6 0.0 all-reduce.11.cloned.1.call-start
  366.6 0.6 all-reduce.11.cloned.1.call-update
  367.1 35.1 %all-reduce.11.cloned.1.call-done = f32[256,64]{0,1:T(8,128)} async-done(((f32[256,64]{0,1:T(8,128)}), f32[256,64]{0,1:T(8,128)}) %all-reduce.11.cloned.1.call-update) | async-done | bytes 65552 | tf_op jit(solution)/shard_map/psum | solution.py:27
  402.2 0.0 copy-done.2
  402.2 0.0 copy-start.4
  402.2 7.9 %subtract_convert_fusion = (bf16[256,4096]{1,0:T(8,128)(2,1)}, f32[256,4096]{1,0:T(8,128)}) fusion(bf16[256,4096]{1,0:T(8,128)(2,1)S(1)} %copy-done.2, f32[256,4096]{1,0:T(8,128)} %param.10, f32[64,4096]{1,0:T(8,128)S(1)} %fusion.12, f32[256,64]{0,1:T(8,128)} %all-reduce.11.cloned.1.call-done), kind=kOutput, calls=%fused_computation.10 | convolution fusion | flops 813711360 | bytes 13697024 | tf_op jit(solution)/shard_map/dot_general | solution.py:29
  410.0 0.0 copy-done.4
  410.0 0.6 copy.15
  (4 shorter events, 0.1 us)
Async XLA Ops:
  7.2 6.0 %copy-start = (f32[256,64]{0,1:T(8,128)S(1)}, f32[256,64]{0,1:T(8,128)}, u32[]{:S(2)}) copy-start(f32[256,64]{0,1:T(8,128)} %param.12) | copy-start | bytes 196612
  7.2 139.0 %all-reduce.5.cloned.1.call-start = ((), (), s32[]{:S(2)}) async-start(), calls=%async_computation | async-start | bytes 2097152 | tf_op jit(solution)/shard_map/psum | solution.py:25
  11.2 2.0 copy-start.1
  17.1 184.6 %all-reduce.7.cloned.1.call-start = ((), (), s32[]{:S(2)}) async-start(), calls=%async_computation.1 | async-start | bytes 262144 | tf_op jit(solution)/shard_map/psum | solution.py:27
  169.0 167.7 %all-reduce.9.cloned.1.call-start = ((), (), s32[]{:S(2)}) async-start(), calls=%async_computation.2 | async-start | bytes 2097152 | tf_op jit(solution)/shard_map/psum | solution.py:25
  359.8 6.8 %copy-start.3 = (f32[256,64]{0,1:T(8,128)}, f32[256,64]{0,1:T(8,128)S(1)}, u32[]{:S(2)}) copy-start(f32[256,64]{0,1:T(8,128)S(1)} %fusion.1) | copy-start | bytes 196612
  359.8 42.4 %copy-start.2 = (bf16[256,4096]{1,0:T(8,128)(2,1)S(1)}, bf16[256,4096]{1,0:T(8,128)(2,1)}, u32[]{:S(2)}) copy-start(bf16[256,4096]{1,0:T(8,128)(2,1)} %param.11) | copy-start | bytes 6291460
  366.6 35.6 %all-reduce.11.cloned.1.call-start = ((), (), s32[]{:S(2)}) async-start(), calls=%async_computation.3 | async-start | bytes 131072 | tf_op jit(solution)/shard_map/psum | solution.py:27
  402.2 7.9 %copy-start.4 = (f32[256,64]{0,1:T(8,128)S(1)}, f32[256,64]{0,1:T(8,128)}, u32[]{:S(2)}) copy-start(f32[256,64]{0,1:T(8,128)} %all-reduce.11.cloned.1.call-done) | copy-start | bytes 196612
Sparse Core Ops, SparseCore 0:
  17.2 128.9 all-reduce.4
  169.1 32.4 all-reduce.6
  207.6 129.0 all-reduce.8
  369.9 32.2 all-reduce.10
where the time goes:
time: 420 us; the launch traced here: 417 us
  waiting for transfers between devices  326 us (78%)
  matrix products  45.8 us (11%)
  other arithmetic  28.1 us (7%)
  between operations  13.9 us (3%)
    psum x2, waiting for transfers between devices, on_device(): factor_rows = orthonormal(lax.psum(partial_value, ('island', 'shard')))  258 us
    psum x2, waiting for transfers between devices, on_device(): basis_now = lax.psum(local_proj, 'island')  67.5 us
    another operation x6, other arithmetic, orthonormal(): lower_factor = jnp.linalg.cholesky(gram_matrix)  13 us
    dot_general x2, matrix products, on_device(): lax.dot_general(merged, factor_rows, (((1,), (1,)), ((), ())), precision=...  11.9 us
    another operation x4, other arithmetic, orthonormal(): lax.linalg.triangular_solve(lower_factor, factor_rows, left_side=True, lo...  11.1 us
    dot_general x2, matrix products, on_device(): lax.dot_general(basis_now, merged, (((0,), (0,)), ((), ())), precision=HIGH)  9.7 us
  transfers between devices with their start and end apart: 4, of which 4 were waited for; matrix products, arithmetic and copies ran while one was open for 0% of the time, Pallas kernels for 0%

commit v1 on v0

v1 whole, which is shorter than its diff:
```python
import functools

import jax
import jax.numpy as jnp
from jax import lax
from jax.experimental import pallas as pl
from jax.experimental.pallas import tpu as pltpu
from jax.sharding import PartitionSpec as P

ITERS = 2

HIGH = lax.Precision.HIGH
HIGHEST = lax.Precision.HIGHEST
outer_beta = 0.9
outer_rate = 0.7
MESH = pl.DeviceIdType.MESH
LANES = 128


def wait_bytes(ref, sem):
    pltpu.make_async_copy(ref, ref, sem).wait()


def reduce_all_kernel(
    n_island, n_shard, p_ref, out_ref, pair_buf, half, terms, pair_send, pair_recv, rs_send, rs_recv, ag_send, ag_recv, fw_send, fw_recv
):
    island, shard = lax.axis_index("island"), lax.axis_index("shard")
    core, row = lax.rem(island, 2), island // 2
    peers = (n_island // 2) * n_shard
    me = row * n_shard + shard
    width = half.shape[1]
    _, rows, cols = terms.shape
    groups = half.shape[0] // rows
    partner = (island + 1 - 2 * core, shard)

    def device(k):
        return ((k // n_shard) * 2 + core, lax.rem(k, n_shard))

    def chunk(ref, k, base):
        start = pl.multiple_of(base + (k // groups) * cols, LANES)
        if groups == 1:
            return ref.at[:, pl.ds(start, cols)]
        return ref.at[pl.ds(pl.multiple_of(lax.rem(k, groups) * rows, 8), rows), pl.ds(start, cols)]

    def each_peer(body):
        @pl.loop(1, peers)
        def _(d):
            body(lax.rem(me + d, peers))

    mine = pl.multiple_of(core * width, LANES)
    other = pl.multiple_of((1 - core) * width, LANES)

    barrier = pltpu.get_barrier_semaphore()
    pl.semaphore_signal(barrier, inc=1, device_id=partner, device_id_type=MESH)
    each_peer(lambda k: pl.semaphore_signal(barrier, inc=1, device_id=device(k), device_id_type=MESH))
    pl.semaphore_wait(barrier, peers)

    pair = pltpu.make_async_remote_copy(
        src_ref=p_ref.at[:, pl.ds(other, width)], dst_ref=pair_buf, send_sem=pair_send, recv_sem=pair_recv, device_id=partner, device_id_type=MESH
    )
    pair.start()
    pair.wait()
    half[...] = p_ref[:, pl.ds(mine, width)] + pair_buf[...]

    def send_term(k):
        pltpu.make_async_remote_copy(
            src_ref=chunk(half, k, 0), dst_ref=terms.at[me], send_sem=rs_send, recv_sem=rs_recv, device_id=device(k), device_id_type=MESH
        ).start()

    each_peer(send_term)
    total = chunk(half, me, 0)[...]
    some = terms.at[pl.ds(0, peers - 1)]
    wait_bytes(some, rs_recv)
    total = lax.fori_loop(1, peers, lambda d, t: t + terms[lax.rem(me + d, peers)], total)
    chunk(out_ref, me, mine)[...] = total
    wait_bytes(some, rs_send)

    def copy_out(k, target, send, recv):
        return pltpu.make_async_remote_copy(
            src_ref=chunk(out_ref, k, mine), dst_ref=chunk(out_ref, k, mine), send_sem=send, recv_sem=recv, device_id=target, device_id_type=MESH
        )

    each_peer(lambda k: copy_out(me, device(k), ag_send, ag_recv.at[me]).start())
    copy_out(me, partner, fw_send, fw_recv).start()

    def forward(k):
        copy_out(k, partner, ag_send, ag_recv.at[k]).wait_recv()
        copy_out(k, partner, fw_send, fw_recv).start()

    each_peer(forward)
    wait_bytes(some, ag_send)
    wait_bytes(half, fw_send)
    wait_bytes(half, fw_recv)


def reduce_all(p, n_island, n_shard, ident):
    rank, dim = p.shape
    peers = (n_island // 2) * n_shard
    width = dim // 2
    groups = max(1, peers * LANES // width)
    rows, cols = rank // groups, width * groups // peers
    f32 = jnp.float32
    sem = pltpu.SemaphoreType.DMA
    return pl.pallas_call(
        functools.partial(reduce_all_kernel, n_island, n_shard),
        out_shape=jax.ShapeDtypeStruct((rank, dim), f32),
        in_specs=[pl.BlockSpec(memory_space=pltpu.VMEM)],
        out_specs=pl.BlockSpec(memory_space=pltpu.VMEM),
        scratch_shapes=[
            pltpu.VMEM((rank, width), f32),
            pltpu.VMEM((rank, width), f32),
            pltpu.VMEM((peers, rows, cols), f32),
            sem, sem, sem, sem, sem, sem((peers,)), sem, sem,
        ],
        compiler_params=pltpu.CompilerParams(collective_id=ident, has_side_effects=True),
        name="reduce_all",
    )(p)


def island_kernel(n_island, x_ref, out_ref, terms, send_sem, recv_sem):
    island, shard = lax.axis_index("island"), lax.axis_index("shard")
    peers = [lax.rem(island + d, n_island) for d in range(1, n_island)]
    barrier = pltpu.get_barrier_semaphore()
    for k in peers:
        pl.semaphore_signal(barrier, inc=1, device_id=(k, shard), device_id_type=MESH)
    pl.semaphore_wait(barrier, n_island - 1)
    copies = [
        pltpu.make_async_remote_copy(
            src_ref=x_ref, dst_ref=terms.at[d], send_sem=send_sem.at[d], recv_sem=recv_sem.at[d], device_id=(k, shard), device_id_type=MESH
        )
        for d, k in enumerate(peers)
    ]
    for copy in copies:
        copy.start()
    total = x_ref[...]
    for copy in copies:
        copy.wait()
    total = None
    for i in range(n_island):
        slot = lax.rem(island - i + n_island, n_island)
        term = jnp.where(slot == 0, x_ref[...], terms[jnp.maximum(slot - 1, 0)])
        total = term if total is None else total + term
    out_ref[...] = total


def reduce_island(x, n_island, ident):
    sem = pltpu.SemaphoreType.DMA
    return pl.pallas_call(
        functools.partial(island_kernel, n_island),
        out_shape=jax.ShapeDtypeStruct(x.shape, jnp.float32),
        in_specs=[pl.BlockSpec(memory_space=pltpu.VMEM)],
        out_specs=pl.BlockSpec(memory_space=pltpu.VMEM),
        scratch_shapes=[pltpu.VMEM((n_island - 1,) + x.shape, jnp.float32), sem((n_island - 1,)), sem((n_island - 1,))],
        compiler_params=pltpu.CompilerParams(collective_id=ident, has_side_effects=True),
        name="reduce_island",
    )(x)


def orthonormal(factor_rows):
    gram_matrix = jnp.dot(factor_rows, factor_rows.T, precision=HIGHEST)
    lower_factor = jnp.linalg.cholesky(gram_matrix)
    return lax.linalg.triangular_solve(lower_factor, factor_rows, left_side=True, lower=True)


def on_device(n_island, n_shard, pseudo_grad, error_buffer, momentum, weights, warm_basis):
    merged = (pseudo_grad + error_buffer)[0]
    basis_rows = warm_basis.T
    for iteration in range(ITERS):
        partial_value = jnp.dot(basis_rows, merged, precision=HIGH)
        factor_rows = orthonormal(reduce_all(partial_value, n_island, n_shard, 0))
        local_rows = lax.dot_general(factor_rows, merged, (((1,), (1,)), ((), ())), precision=HIGH)
        basis_rows = reduce_island(local_rows, n_island, 1)
    new_error = merged - jnp.dot(local_rows.T, factor_rows, precision=HIGH)
    update = jnp.dot(basis_rows.T / n_island, factor_rows, precision=HIGH)
    new_momentum = outer_beta * momentum + update
    stepped = weights.astype(jnp.float32) - outer_rate * (update + outer_beta * new_momentum)
    return (new_error[None], new_momentum, stepped.astype(jnp.bfloat16), basis_rows.T)


def solution(mesh):
    in_specs = (
        P("island", "shard", None),
        P("island", "shard", None),
        P("shard", None),
        P("shard", None),
        P("shard", None),
    )
    out_specs = (P("island", "shard", None), P("shard", None), P("shard", None), P("shard", None))
    body = functools.partial(on_device, mesh.shape["island"], mesh.shape["shard"])
    return jax.shard_map(body, mesh=mesh, in_specs=in_specs, out_specs=out_specs, check_vma=False)
```

time: 420 us -> 155 us (0.37)
  waiting for transfers between devices: 326 us -> 0 us
  Pallas kernels: 0 us -> 85.3 us
  between operations: 13.9 us -> 0.81 us
  matrix products: 45.8 us -> 37.3 us
    psum x4 -> x0, waiting for transfers between devices: 326 us -> none  [the longest x2 258 us: on_device(): factor_rows = orthonormal(lax.psum(partial_value, ('island', 'shard')))]
    pallas_call x0 -> x4, Pallas kernels: none -> 85.3 us  [the longest x2 71.7 us: reduce_all(): pl.pallas_call(functools.partial(reduce_all_kernel, n_island, n_shard), o...]
    dot_general x8, matrix products: 41.3 us -> 32.7 us  [the longest x2 9.09 us: on_device(): lax.dot_general(factor_rows, merged, (((1,), (1,)), ((), ())), precision=...]
  transfers between devices with their start and end apart: 4 -> 0, of which waited for: 4 -> 0; matrix products, arithmetic and copies ran while one was open for 0% -> 0% of each run, Pallas kernels for 0% -> 0%
where the time goes in v1:
time: 155 us; the launch traced here: 154 us
  Pallas kernels  85.3 us (55%)
  matrix products  37.3 us (24%)
  other arithmetic  28.1 us (18%)
  local copies, waits for them, and re-layouts  2.83 us (2%)
    pallas_call x2, Pallas kernels, reduce_all(): pl.pallas_call(functools.partial(reduce_all_kernel, n_island, n_shard), o...  71.7 us
    pallas_call x2, Pallas kernels, reduce_island(): pl.pallas_call(functools.partial(island_kernel, n_island), out_shape=jax....  13.6 us
    another operation x6, other arithmetic, orthonormal(): lower_factor = jnp.linalg.cholesky(gram_matrix)  13 us
    another operation x4, other arithmetic, orthonormal(): lax.linalg.triangular_solve(lower_factor, factor_rows, left_side=True, lo...  11.1 us
    dot_general x2, matrix products, on_device(): lax.dot_general(factor_rows, merged, (((1,), (1,)), ((), ())), precision=...  9.09 us
    dot_general x1, matrix products, on_device(): update = jnp.dot(basis_rows.T / n_island, factor_rows, precision=HIGH)  7.65 us
    dot_general x2, matrix products, on_device(): partial_value = jnp.dot(basis_rows, merged, precision=HIGH)  6.94 us
    dot_general x2, matrix products, orthonormal(): gram_matrix = jnp.dot(factor_rows, factor_rows.T, precision=HIGHEST)  5.04 us

profile of v1, /device:TPU:25, one launch (start us, length us, event | category | flops | bytes accessed | tf_op | source)
XLA Modules:
  0.0 154.4 jit_solution(15035702397947685456)
XLA Ops:
  0.6 0.0 copy-start
  0.6 4.0 %add.17 = f32[1,256,4096]{2,1,0:T(8,128)S(1)} add(f32[1,256,4096]{2,1,0:T(8,128)} %param.8, f32[1,256,4096]{2,1,0:T(8,128)} %param.9) | non-fusion elementwise | flops 1048576 | bytes 12582912 | tf_op jit(solution)/shard_map/add | solution.py:166
  4.6 0.0 copy-start.1
  4.6 2.0 %copy-done.1 = f32[1,256,4096]{2,1,0:T(8,128)} copy-done((f32[1,256,4096]{2,1,0:T(8,128)}, f32[1,256,4096]{2,1,0:T(8,128)S(1)}, u32[]{:S(2)}) %copy-start.1) | copy-done | bytes 4194328
  6.6 0.0 copy-done
  6.6 2.3 %convolution_bitcast_fusion.p_ref = f32[64,4096]{1,0:T(8,128)} fusion(f32[256,64]{0,1:T(8,128)S(1)} %copy-done, f32[1,256,4096]{2,1,0:T(8,128)S(1)} %add.17), kind=kOutput, calls=%fused_computation.2 | convolution fusion | flops 402653184 | bytes 5308416 | tf_op jit(solution)/shard_map/dot_general | solution.py:169
  9.0 36.6 %reduce_all.2 = f32[64,4096]{1,0:T(8,128)} custom-call(f32[64,4096]{1,0:T(8,128)} %convolution_bitcast_fusion.p_ref), custom_call_target="tpu_custom_call" | custom-call | tf_op jit(solution)/shard_map/reduce_all/pallas_call | solution.py:104
  45.6 2.5 %fusion.22 = f32[64,64]{1,0:T(8,128)S(1)} fusion(f32[64,4096]{1,0:T(8,128)} %reduce_all.2), kind=kOutput, calls=%fused_computation.35 | convolution fusion | flops 201326592 | bytes 1064960 | tf_op jit(solution)/shard_map/dot_general | solution.py:160
  48.1 0.1 copy.9
  48.2 5.8 %cholesky.44 = f32[64,64]{1,0:T(8,128)S(1)} custom-call(f32[64,64]{1,0:T(8,128)S(1)} %fusion.17), custom_call_target="Cholesky" | custom-call | tf_op jit(solution)/shard_map/jit(cholesky)/cholesky | solution.py:161
  54.1 0.6 compare_reduce_fusion.1
  54.7 0.7 fusion.10
  55.4 4.9 %custom-call.6 = f32[1,64,64]{1,2,0:T(8,128)S(1)} custom-call(f32[1,64,64]{2,1,0:T(8,128)S(1)} %fusion.10), custom_call_target="InvertDiagBlocksLowerTriangular" | custom-call | tf_op jit(solution)/shard_map/triangular_solve/custom-call.0 | solution.py:162
  60.3 2.3 %fusion.15 = f32[64,4096]{1,0:T(8,128)S(1)} fusion(f32[64,4096]{1,0:T(8,128)} %reduce_all.2, f32[1,64,64]{1,2,0:T(8,128)S(1)} %custom-call.6), kind=kOutput, calls=%fused_computation.22 | convolution fusion | flops 201326592 | bytes 2113536 | tf_op jit(solution)/shard_map/triangular_solve/dot.1 | solution.py:162
  62.5 4.9 %fusion.5.x_ref = f32[64,256]{1,0:T(8,128)} fusion(f32[64,4096]{1,0:T(8,128)S(1)} %fusion.15, f32[1,256,4096]{2,1,0:T(8,128)} %copy-done.1), kind=kOutput, calls=%fused_computation.7 | convolution fusion | flops 402653184 | bytes 5308416 | tf_op jit(solution)/shard_map/dot_general | solution.py:171
  67.4 6.8 %reduce_island.2 = f32[64,256]{1,0:T(8,128)} custom-call(f32[64,256]{1,0:T(8,128)} %fusion.5.x_ref), custom_call_target="tpu_custom_call" | custom-call | tf_op jit(solution)/shard_map/reduce_island/pallas_call | solution.py:148
  74.2 4.6 %fusion.3.p_ref = f32[64,4096]{1,0:T(8,128)} fusion(f32[64,256]{1,0:T(8,128)} %reduce_island.2, f32[1,256,4096]{2,1,0:T(8,128)} %copy-done.1), kind=kOutput, calls=%fused_computation.5 | convolution fusion | flops 402653184 | bytes 5308416 | tf_op jit(solution)/shard_map/dot_general | solution.py:169
  78.8 35.1 %reduce_all.3 = f32[64,4096]{1,0:T(8,128)} custom-call(f32[64,4096]{1,0:T(8,128)} %fusion.3.p_ref), custom_call_target="tpu_custom_call" | custom-call | tf_op jit(solution)/shard_map/reduce_all/pallas_call | solution.py:104
  114.0 2.5 %fusion.23 = f32[64,64]{1,0:T(8,128)S(1)} fusion(f32[64,4096]{1,0:T(8,128)} %reduce_all.3), kind=kOutput, calls=%fused_computation.36 | convolution fusion | flops 201326592 | bytes 1064960 | tf_op jit(solution)/shard_map/dot_general | solution.py:160
  116.5 0.1 copy.10
  116.6 5.8 %cholesky.55 = f32[64,64]{1,0:T(8,128)S(1)} custom-call(f32[64,64]{1,0:T(8,128)S(1)} %fusion.14), custom_call_target="Cholesky" | custom-call | tf_op jit(solution)/shard_map/jit(cholesky)/cholesky | solution.py:161
  122.5 0.6 compare_reduce_fusion
  123.1 0.7 fusion.11
  123.8 4.9 %custom-call.7 = f32[1,64,64]{1,2,0:T(8,128)S(1)} custom-call(f32[1,64,64]{2,1,0:T(8,128)S(1)} %fusion.11), custom_call_target="InvertDiagBlocksLowerTriangular" | custom-call | tf_op jit(solution)/shard_map/triangular_solve/custom-call.0 | solution.py:162
  128.7 0.0 copy-start.2
  128.7 2.4 %fusion.12 = f32[64,4096]{1,0:T(8,128)S(1)} fusion(f32[64,4096]{1,0:T(8,128)} %reduce_all.3, f32[1,64,64]{1,2,0:T(8,128)S(1)} %custom-call.7), kind=kOutput, calls=%fused_computation.18 | convolution fusion | flops 201326592 | bytes 2113536 | tf_op jit(solution)/shard_map/triangular_solve/dot.1 | solution.py:162
  131.1 4.2 %fusion.1.x_ref = f32[64,256]{1,0:T(8,128)S(1)} fusion(f32[64,4096]{1,0:T(8,128)S(1)} %fusion.12, f32[1,256,4096]{2,1,0:T(8,128)} %copy-done.1), kind=kOutput, calls=%fused_computation.3 | convolution fusion | flops 402653184 | bytes 5308416 | tf_op jit(solution)/shard_map/dot_general | solution.py:171
  135.3 0.0 copy-done.2
  135.3 0.0 copy-start.5
  135.3 0.0 copy-start.3
  135.3 3.9 %fusion = f32[1,256,4096]{2,1,0:T(8,128)} fusion(f32[64,256]{1,0:T(8,128)S(1)} %fusion.1.x_ref, f32[64,4096]{1,0:T(8,128)S(1)} %fusion.12, f32[1,256,4096]{2,1,0:T(8,128)S(1)} %copy-done.2), kind=kOutput, calls=%fused_computation.1 | convolution fusion | flops 403701760 | bytes 9502720 | tf_op jit(solution)/shard_map/dot_general | solution.py:173
  139.3 0.0 copy-done.5
  139.3 6.8 %reduce_island.3 = f32[64,256]{1,0:T(8,128)} custom-call(f32[64,256]{1,0:T(8,128)} %copy-done.5), custom_call_target="tpu_custom_call" | custom-call | tf_op jit(solution)/shard_map/reduce_island/pallas_call | solution.py:148
  146.1 0.0 copy-done.3
  146.1 0.0 copy-start.4
  146.1 7.7 %subtract_convert_fusion = (bf16[256,4096]{1,0:T(8,128)(2,1)}, f32[256,4096]{1,0:T(8,128)}) fusion(bf16[256,4096]{1,0:T(8,128)(2,1)S(1)} %copy-done.3, f32[256,4096]{1,0:T(8,128)} %param.10, f32[64,4096]{1,0:T(8,128)S(1)} %fusion.12, f32[256,64]{0,1:T(8,128)} %bitcast.46), kind=kOutput, calls=%fused_computation.10 | convolution fusion | flops 411058176 | bytes 13697024 | tf_op jit(solution)/shard_map/dot_general | solution.py:174
  153.7 0.0 copy-done.4
  153.7 0.6 copy.12
  (4 shorter events, 0.1 us)
Async XLA Ops:
  0.6 6.0 %copy-start = (f32[256,64]{0,1:T(8,128)S(1)}, f32[256,64]{0,1:T(8,128)}, u32[]{:S(2)}) copy-start(f32[256,64]{0,1:T(8,128)} %param.12) | copy-start | bytes 196612
  4.6 2.0 %copy-start.1 = (f32[1,256,4096]{2,1,0:T(8,128)}, f32[1,256,4096]{2,1,0:T(8,128)S(1)}, u32[]{:S(2)}) copy-start(f32[1,256,4096]{2,1,0:T(8,128)S(1)} %add.17) | copy-start | bytes 12582916
  128.7 6.7 %copy-start.2 = (f32[1,256,4096]{2,1,0:T(8,128)S(1)}, f32[1,256,4096]{2,1,0:T(8,128)}, u32[]{:S(2)}) copy-start(f32[1,256,4096]{2,1,0:T(8,128)} %copy-done.1) | copy-start | bytes 12582916
  135.3 4.0 %copy-start.5 = (f32[64,256]{1,0:T(8,128)}, f32[64,256]{1,0:T(8,128)S(1)}, u32[]{:S(2)}) copy-start(f32[64,256]{1,0:T(8,128)S(1)} %fusion.1.x_ref) | copy-start | bytes 196612
  135.3 10.7 %copy-start.3 = (bf16[256,4096]{1,0:T(8,128)(2,1)S(1)}, bf16[256,4096]{1,0:T(8,128)(2,1)}, u32[]{:S(2)}) copy-start(bf16[256,4096]{1,0:T(8,128)(2,1)} %param.11) | copy-start | bytes 6291460
  146.1 7.7 %copy-start.4 = (f32[64,256]{1,0:T(8,128)S(1)}, f32[64,256]{1,0:T(8,128)}, u32[]{:S(2)}) copy-start(f32[64,256]{1,0:T(8,128)} %reduce_island.3) | copy-start | bytes 196612

commit v2 on v1

--- a/solution.py
+++ b/solution.py
@@ -156,10 +156,43 @@
     )(x)
 
 
+def orthonormal_kernel(p_ref, out_ref):
+    p = p_ref[...]
+    rank = p.shape[0]
+    gram = lax.dot_general(p, p, (((1,), (1,)), ((), ())), precision=HIGHEST, preferred_element_type=jnp.float32)
+    step = 8
+    tiles = rank // step
+    left = [gram[t * step : (t + 1) * step] for t in range(tiles)]
+    row_id = lax.broadcasted_iota(jnp.int32, (step, rank), 0)
+    col_id = lax.broadcasted_iota(jnp.int32, (step, rank), 1)
+    diagonal = [row_id + t * step == col_id for t in range(tiles)]
+    right = [jnp.where(d, 1.0, 0.0) for d in diagonal]
+    for j in range(rank):
+        t, s = divmod(j, step)
+        row, side = left[t][s : s + 1], right[t][s : s + 1]
+        row_over = row / left[t][s : s + 1, j : j + 1]
+        side_over = side / left[t][s : s + 1, j : j + 1]
+        for u in range(t, tiles):
+            col = left[u][:, j : j + 1]
+            if u == t:
+                col = jnp.where(row_id[:, :1] > s, col, 0.0)
+            left[u] = left[u] - col * row_over
+            right[u] = right[u] - col * side_over
+    for t in range(tiles):
+        pivot = jnp.sum(jnp.where(diagonal[t], left[t], 0.0), axis=1, keepdims=True)
+        right[t] = right[t] / jnp.sqrt(pivot)
+    inverse = jnp.concatenate(right, axis=0)
+    out_ref[...] = jnp.dot(inverse, p, precision=HIGHEST, preferred_element_type=jnp.float32)
+
+
 def orthonormal(factor_rows):
-    gram_matrix = jnp.dot(factor_rows, factor_rows.T, precision=HIGHEST)
-    lower_factor = jnp.linalg.cholesky(gram_matrix)
-    return lax.linalg.triangular_solve(lower_factor, factor_rows, left_side=True, lower=True)
+    return pl.pallas_call(
+        orthonormal_kernel,
+        out_shape=jax.ShapeDtypeStruct(factor_rows.shape, jnp.float32),
+        in_specs=[pl.BlockSpec(memory_space=pltpu.VMEM)],
+        out_specs=pl.BlockSpec(memory_space=pltpu.VMEM),
+        name="orthonormal",
+    )(factor_rows)
 
 
 def on_device(n_island, n_shard, pseudo_grad, error_buffer, momentum, weights, warm_basis):

time: 155 us -> 143 us (0.923)
  other arithmetic: 28.1 us -> 3.97 us
  Pallas kernels: 85.3 us -> 107 us
  matrix products: 37.3 us -> 28.4 us
    another operation x10 -> x0, other arithmetic: 24.1 us -> none  [the longest x6 13 us: orthonormal(): lower_factor = jnp.linalg.cholesky(gram_matrix)]
    pallas_call x0 -> x2, Pallas kernels: none -> 22.1 us  [orthonormal(): pl.pallas_call(orthonormal_kernel, out_shape=jax.ShapeDtypeStruct(factor_...]
    dot_general x2 -> x0, matrix products: 5.04 us -> none  [orthonormal(): gram_matrix = jnp.dot(factor_rows, factor_rows.T, precision=HIGHEST)]
    another operation x2 -> x0, matrix products: 4.67 us -> none  [orthonormal(): lax.linalg.triangular_solve(lower_factor, factor_rows, left_side=True, lo...]
where the time goes in v2:
time: 143 us
  Pallas kernels  107 us (75%)
  matrix products  28.4 us (20%)
  other arithmetic  3.97 us (3%)
  local copies, waits for them, and re-layouts  2.67 us (2%)
    pallas_call x2, Pallas kernels, reduce_all(): pl.pallas_call(functools.partial(reduce_all_kernel, n_island, n_shard), o...  71.7 us
    pallas_call x2, Pallas kernels, orthonormal(): pl.pallas_call(orthonormal_kernel, out_shape=jax.ShapeDtypeStruct(factor_...  22.1 us
    pallas_call x2, Pallas kernels, reduce_island(): pl.pallas_call(functools.partial(island_kernel, n_island), out_shape=jax....  13.6 us
    dot_general x2, matrix products, on_device(): lax.dot_general(factor_rows, merged, (((1,), (1,)), ((), ())), precision=...  9.87 us
    dot_general x1, matrix products, on_device(): update = jnp.dot(basis_rows.T / n_island, factor_rows, precision=HIGH)  7.66 us
    dot_general x2, matrix products, on_device(): partial_value = jnp.dot(basis_rows, merged, precision=HIGH)  6.93 us
    add x1, other arithmetic, on_device(): merged = (pseudo_grad + error_buffer)[0]  3.97 us
    dot_general x1, matrix products, on_device(): new_error = merged - jnp.dot(local_rows.T, factor_rows, precision=HIGH)  3.94 us

profile of v2, /device:TPU:25, one launch (start us, length us, event | category | flops | bytes accessed | tf_op | source)
XLA Modules:
  0.0 143.1 jit_solution(9510951853151665066)
XLA Ops:
  0.6 0.0 copy-start
  0.6 4.0 %add.9 = f32[1,256,4096]{2,1,0:T(8,128)S(1)} add(f32[1,256,4096]{2,1,0:T(8,128)} %param.5, f32[1,256,4096]{2,1,0:T(8,128)} %param.6) | non-fusion elementwise | flops 1048576 | bytes 12582912 | tf_op jit(solution)/shard_map/add | solution.py:199
  4.6 0.0 copy-start.1
  4.6 2.0 %copy-done.1 = f32[1,256,4096]{2,1,0:T(8,128)} copy-done((f32[1,256,4096]{2,1,0:T(8,128)}, f32[1,256,4096]{2,1,0:T(8,128)S(1)}, u32[]{:S(2)}) %copy-start.1) | copy-done | bytes 4194328
  6.6 0.0 copy-done
  6.6 2.3 %convolution_bitcast_fusion.p_ref = f32[64,4096]{1,0:T(8,128)} fusion(f32[256,64]{0,1:T(8,128)S(1)} %copy-done, f32[1,256,4096]{2,1,0:T(8,128)S(1)} %add.9), kind=kOutput, calls=%fused_computation.2 | convolution fusion | flops 402653184 | bytes 5308416 | tf_op jit(solution)/shard_map/dot_general | solution.py:202
  9.0 36.6 %reduce_all.2.p_ref = f32[64,4096]{1,0:T(8,128)} custom-call(f32[64,4096]{1,0:T(8,128)} %convolution_bitcast_fusion.p_ref), custom_call_target="tpu_custom_call" | custom-call | tf_op jit(solution)/shard_map/reduce_all/pallas_call | solution.py:104
  45.5 11.0 %orthonormal.2 = f32[64,4096]{1,0:T(8,128)} custom-call(f32[64,4096]{1,0:T(8,128)} %reduce_all.2.p_ref), custom_call_target="tpu_custom_call" | custom-call | tf_op jit(solution)/shard_map/orthonormal/pallas_call | solution.py:189
  56.6 5.2 %fusion.5.x_ref = f32[64,256]{1,0:T(8,128)} fusion(f32[64,4096]{1,0:T(8,128)} %orthonormal.2, f32[1,256,4096]{2,1,0:T(8,128)} %copy-done.1), kind=kOutput, calls=%fused_computation.7 | convolution fusion | flops 402653184 | bytes 5308416 | tf_op jit(solution)/shard_map/dot_general | solution.py:204
  61.8 6.8 %reduce_island.2 = f32[64,256]{1,0:T(8,128)} custom-call(f32[64,256]{1,0:T(8,128)} %fusion.5.x_ref), custom_call_target="tpu_custom_call" | custom-call | tf_op jit(solution)/shard_map/reduce_island/pallas_call | solution.py:148
  68.5 4.6 %fusion.3.p_ref = f32[64,4096]{1,0:T(8,128)} fusion(f32[64,256]{1,0:T(8,128)} %reduce_island.2, f32[1,256,4096]{2,1,0:T(8,128)} %copy-done.1), kind=kOutput, calls=%fused_computation.5 | convolution fusion | flops 402653184 | bytes 5308416 | tf_op jit(solution)/shard_map/dot_general | solution.py:202
  73.2 35.1 %reduce_all.3.p_ref = f32[64,4096]{1,0:T(8,128)} custom-call(f32[64,4096]{1,0:T(8,128)} %fusion.3.p_ref), custom_call_target="tpu_custom_call" | custom-call | tf_op jit(solution)/shard_map/reduce_all/pallas_call | solution.py:104
  108.3 11.0 %orthonormal.3 = f32[64,4096]{1,0:T(8,128)} custom-call(f32[64,4096]{1,0:T(8,128)} %reduce_all.3.p_ref), custom_call_target="tpu_custom_call" | custom-call | tf_op jit(solution)/shard_map/orthonormal/pallas_call | solution.py:189
  119.3 0.0 copy-start.2
  119.3 0.0 copy-start.3
  119.3 4.7 %fusion.1.x_ref = f32[64,256]{1,0:T(8,128)S(1)} fusion(f32[64,4096]{1,0:T(8,128)} %orthonormal.3, f32[1,256,4096]{2,1,0:T(8,128)} %copy-done.1), kind=kOutput, calls=%fused_computation.3 | convolution fusion | flops 402653184 | bytes 5308416 | tf_op jit(solution)/shard_map/dot_general | solution.py:204
  124.0 0.0 copy-done.2
  124.0 0.0 copy-done.3
  124.0 0.0 copy-start.6
  124.0 0.0 copy-start.4
  124.0 3.9 %fusion = f32[1,256,4096]{2,1,0:T(8,128)} fusion(f32[64,256]{1,0:T(8,128)S(1)} %fusion.1.x_ref, f32[64,4096]{1,0:T(8,128)S(1)} %copy-done.3, f32[1,256,4096]{2,1,0:T(8,128)S(1)} %copy-done.2), kind=kOutput, calls=%fused_computation.1 | convolution fusion | flops 403701760 | bytes 9502720 | tf_op jit(solution)/shard_map/dot_general | solution.py:206
  128.0 0.0 copy-done.6
  128.0 6.8 %reduce_island.3 = f32[64,256]{1,0:T(8,128)} custom-call(f32[64,256]{1,0:T(8,128)} %copy-done.6), custom_call_target="tpu_custom_call" | custom-call | tf_op jit(solution)/shard_map/reduce_island/pallas_call | solution.py:148
  134.8 0.0 copy-done.4
  134.8 0.0 copy-start.5
  134.8 7.7 %subtract_convert_fusion = (bf16[256,4096]{1,0:T(8,128)(2,1)}, f32[256,4096]{1,0:T(8,128)}) fusion(bf16[256,4096]{1,0:T(8,128)(2,1)S(1)} %copy-done.4, f32[256,4096]{1,0:T(8,128)} %param.7, f32[64,4096]{1,0:T(8,128)S(1)} %copy-done.3, f32[256,64]{0,1:T(8,128)} %bitcast.22), kind=kOutput, calls=%fused_computation.10 | convolution fusion | flops 411058176 | bytes 13697024 | tf_op jit(solution)/shard_map/dot_general | solution.py:207
  142.5 0.0 copy-done.5
  142.5 0.6 copy.10
Async XLA Ops:
  0.6 6.0 %copy-start = (f32[256,64]{0,1:T(8,128)S(1)}, f32[256,64]{0,1:T(8,128)}, u32[]{:S(2)}) copy-start(f32[256,64]{0,1:T(8,128)} %param.9) | copy-start | bytes 196612
  4.6 2.0 %copy-start.1 = (f32[1,256,4096]{2,1,0:T(8,128)}, f32[1,256,4096]{2,1,0:T(8,128)S(1)}, u32[]{:S(2)}) copy-start(f32[1,256,4096]{2,1,0:T(8,128)S(1)} %add.9) | copy-start | bytes 12582916
  119.3 4.7 %copy-start.2 = (f32[1,256,4096]{2,1,0:T(8,128)S(1)}, f32[1,256,4096]{2,1,0:T(8,128)}, u32[]{:S(2)}) copy-start(f32[1,256,4096]{2,1,0:T(8,128)} %copy-done.1) | copy-start | bytes 12582916
  119.3 4.7 %copy-start.3 = (f32[64,4096]{1,0:T(8,128)S(1)}, f32[64,4096]{1,0:T(8,128)}, u32[]{:S(2)}) copy-start(f32[64,4096]{1,0:T(8,128)} %orthonormal.3) | copy-start | bytes 3145732
  124.0 4.0 %copy-start.6 = (f32[64,256]{1,0:T(8,128)}, f32[64,256]{1,0:T(8,128)S(1)}, u32[]{:S(2)}) copy-start(f32[64,256]{1,0:T(8,128)S(1)} %fusion.1.x_ref) | copy-start | bytes 196612
  124.0 10.7 %copy-start.4 = (bf16[256,4096]{1,0:T(8,128)(2,1)S(1)}, bf16[256,4096]{1,0:T(8,128)(2,1)}, u32[]{:S(2)}) copy-start(bf16[256,4096]{1,0:T(8,128)(2,1)} %param.8) | copy-start | bytes 6291460
  134.8 7.7 %copy-start.5 = (f32[64,256]{1,0:T(8,128)S(1)}, f32[64,256]{1,0:T(8,128)}, u32[]{:S(2)}) copy-start(f32[64,256]{1,0:T(8,128)} %reduce_island.3) | copy-start | bytes 196612
